TPU v7x, 256 devices: a 4x2x16 block of a 4x16x16 slice. The times are simulated.
256 devices in a mesh: cosmo: 2 (over y), shell: 4 (over x), band: 32 (over z, core).
Axes of the slice: x: 4, y: 2, z: 16, core: 2. Of those that a mesh axis runs over, the one named last changes fastest.
The devices are a block of a 4x16x16 slice.
Arguments:
- cycle_modes: float32 [1024, 128, 2, 128], P(('cosmo', 'shell'), 'band'), parts along dimension 0, may hold values from -6 to 6
- cycle_weight: float32 [128], P('band'), may hold values from 0.5 to 2
- legendre: float32 [128, 128, 4096], P('band'), may hold values from -0.5 to 0.5
- spin_plus: bfloat16 [128, 128, 4096], P('band'), may hold values from -0.5 to 0.5
- spin_minus: bfloat16 [128, 128, 4096], P('band'), may hold values from -0.5 to 0.5
- window: float32 [512, 4096], P('shell'), may hold values from 0.3 to 3
- lensing: float32 [1024], P(('cosmo', 'shell')), parts along dimension 0, may hold values from 0.05 to 0.5
- source_shell: int32 [8], P('cosmo'), parts along dimension 0, may hold values from 384 to 511
Outputs:
- lensing_maps: float32 [8, 3, 128, 2, 128], P(('cosmo', 'shell'), None, 'band'), parts along dimension 0
There are 2 independent parts, one for each index of `cosmo`. A program takes and returns all parts, laid end to end along the dimension named above; an argument that names none is the same for every part. Nothing has to cross between parts.
All inputs are finite; a program needn't handle non-finite values.
Results may differ from a plain program's by a relative error of at most 0.00073.
Values sent between devices are 32-bit elements; how exact they have to be, the bound alone decides.
A program may use at most 64 MiB of HBM per device.

v0:
```python
import jax
import jax.numpy as jnp
from jax import lax
from jax.sharding import Mesh
from jax.sharding import PartitionSpec as P

BAND = ("band_0", "band_1")


def cut_along(shard, dim, size):
    before, after = (shard.shape[:dim], shard.shape[dim + 1 :])
    return jnp.moveaxis(shard.reshape(*before, size, -1, *after), dim, 0)


def sent_and_summed(shard, axis, dim):
    size = lax.axis_size(axis)
    tiles = lax.all_to_all(cut_along(shard, dim, size), axis, 0, 0, tiled=True)
    return jnp.sum(tiles, axis=0)


def laid_out(tiles, dim):
    dims = list(tiles.shape[1:])
    dims[dim] *= tiles.shape[0]
    return jnp.moveaxis(tiles, 0, dim).reshape(dims)


def exchange_in_order(tiles, axes, order):
    dims = [lax.axis_size(a) for a in axes]
    tiles = tiles.reshape(*dims, *tiles.shape[1:])
    for k in order:
        tiles = lax.all_to_all(tiles, axes[k], split_axis=k, concat_axis=k, tiled=True)
    return tiles.reshape(-1, *tiles.shape[len(axes) :])


def two_step_exchange(shard, groups, order, split_dim, concat_dim):
    size = lax.axis_size(groups[0]) * lax.axis_size(groups[1])
    tiles = cut_along(shard, split_dim, size)
    return laid_out(exchange_in_order(tiles, groups, order), concat_dim)


def on_device(
    cycle_modes, cycle_weight, legendre, spin_plus, spin_minus, window, lensing, source_shell
):
    highest = lax.Precision.HIGHEST
    weighted = cycle_modes * cycle_weight[None, :, None, None]
    harmonic = jnp.einsum(
        "nrcm,mrl->nmcl",
        lax.all_to_all(weighted, BAND, split_axis=3, concat_axis=1, tiled=True),
        legendre,
        precision=highest,
        preferred_element_type=jnp.float32,
    )
    local_shells = window.shape[0]
    degrees = legendre.shape[2]
    degree = jnp.arange(degrees).astype(jnp.float32)
    shell_ids = lax.axis_index("shell") * local_shells + jnp.arange(local_shells)
    efficiency = (
        lensing[None, :]
        * jnp.maximum(source_shell[:, None] - shell_ids[None, :], 0).astype(jnp.float32)
        / (source_shell[:, None] + 1).astype(jnp.float32)
    )
    binned = jnp.einsum(
        "bs,smcl->bmcl", efficiency, harmonic * window[:, None, None, :], precision=highest
    )
    shear_ratio = jnp.where(
        degree >= 2.0,
        jnp.sqrt((degree + 2.0) * (degree - 1.0) / jnp.maximum(degree * (degree + 1.0), 1.0)),
        0.0,
    )
    shear_coef = (-shear_ratio[None, None, None, :] * binned).astype(jnp.bfloat16)
    kappa_map = jnp.einsum(
        "bmcl,mrl->brcm", binned, legendre, precision=highest, preferred_element_type=jnp.float32
    )
    plus_map = jnp.einsum(
        "bmcl,mrl->brcm", shear_coef, spin_plus, preferred_element_type=jnp.float32
    )
    minus_map = jnp.einsum(
        "bmcl,mrl->brcm", shear_coef, spin_minus, preferred_element_type=jnp.float32
    )
    rotated = jnp.stack([-minus_map[:, :, 1], minus_map[:, :, 0]], axis=2)
    fields = jnp.stack([kappa_map, plus_map, rotated], axis=1)
    owned = sent_and_summed(fields, "shell", 0)
    return two_step_exchange(owned, ("band_0", "band_1"), (1, 0), 2, 4)


def solution(mesh):
    torus = Mesh(
        mesh.devices.reshape(mesh.shape["cosmo"], mesh.shape["shell"], 16, 2),
        ("cosmo", "shell", "band_0", "band_1"),
    )
    in_specs = (
        P(("cosmo", "shell"), BAND, None, None),
        P(BAND),
        P(BAND, None, None),
        P(BAND, None, None),
        P(BAND, None, None),
        P("shell", None),
        P(("cosmo", "shell")),
        P("cosmo"),
    )
    out_specs = P(("cosmo", "shell"), None, BAND, None, None)
    return jax.shard_map(
        on_device, mesh=torus, in_specs=in_specs, out_specs=out_specs, check_vma=False
    )
```

profile of v0, /device:TPU:33, one launch (start us, length us, event | category | flops | bytes accessed | tf_op | source)
XLA Modules:
  0.0 131.3 jit_solution(2260566950642712004)
XLA Ops:
  0.0 1.2 copy_multiply_fusion
  1.2 1.0 copy.32
  2.2 25.5 %all-to-all-start = ((f32[128,4,2,128]{0,2,1,3:T(2,128)}), f32[128,4,2,128]{0,2,1,3:T(2,128)S(1)}, u32[]{:S(2)}, u32[]{:S(2)}) async-start(f32[128,4,2,128]{0,2,1,3:T(2,128)} %copy.32), calls=%async_computation | async-start | bytes 1048576 | tf_op jit(solution)/shard_map/all_to_all | solution.py:48
  27.7 0.7 add_convert_fusion
  28.4 32.6 %all-to-all-done = f32[128,4,2,128]{0,2,1,3:T(2,128)S(1)} async-done(((f32[128,4,2,128]{0,2,1,3:T(2,128)}), f32[128,4,2,128]{0,2,1,3:T(2,128)S(1)}, u32[]{:S(2)}, u32[]{:S(2)}) %all-to-all-start) | async-done | bytes 524320 | tf_op jit(solution)/shard_map/all_to_all | solution.py:48
  61.1 0.3 copy.34
  61.5 16.2 %fusion.5 = f32[4,128,2,4096]{3,1,2,0:T(8,128)S(1)} fusion(f32[4,128,4096]{2,1,0:T(8,128)} %param.10, f32[128,128,2,4]{0,1,3,2:T(8,128)S(1)} %bitcast.66), kind=kOutput, calls=%fused_computation.5 | convolution fusion | flops 6442450944 | bytes 25690112 | tf_op jit(solution)/shard_map/nrcm,mrl->nmcl/dot_general | solution.py:46
  77.7 8.5 %fusion = f32[4,4,2,4096]{3,0,2,1:T(4,128)S(1)} fusion(f32[4,128,2,4096]{3,1,2,0:T(8,128)S(1)} %fusion.5, f32[128,4096]{1,0:T(8,128)S(1)} %copy-done, f32[4]{0:T(128)S(1)} %add_convert_fusion, s32[128]{0:T(128)S(1)} %iota_add_fusion, s32[4]{0:T(128)S(1)} %copy-done.3, f32[128]{0:T(128)S(1)} %copy-done.4), kind=kOutput, calls=%fused_computation | convolution fusion | flops 205523456 | bytes 19399712 | tf_op jit(solution)/shard_map/bs,smcl->bmcl/dot_general | solution.py:62
  86.3 7.6 %fusion.12 = f32[4,1,128,2,4]{2,0,3,4,1:T(4,128)S(1)} fusion(f32[4,4,2,4096]{3,0,2,1:T(4,128)S(1)} %fusion, f32[4,128,4096]{2,1,0:T(8,128)S(1)} %bitcast.65), kind=kOutput, calls=%fused_computation.12 | convolution fusion | flops 201326592 | bytes 8929280 | tf_op jit(solution)/shard_map/bmcl,mrl->brcm/dot_general | solution.py:71
  93.8 1.3 fusion.18
  95.2 1.3 fusion.15
  96.5 8.5 %all_to_all.33 = f32[4,1,3,128,2,4]{3,4,5,2,1,0:T(2,128)S(1)} all-to-all(f32[4,1,3,128,2,4]{3,4,5,2,1,0:T(2,128)S(1)} %copy.36), channel_id=1, replica_groups=mesh['cosmo'=2,'shell'=4,'band_0'=16,'band_1'=2] {'shell'}, dimensions={0} | all-to-all | bytes 98304 | tf_op jit(solution)/shard_map/all_to_all | solution.py:17
  105.1 0.4 reshape.45
  105.5 0.4 copy.39
  106.0 5.3 %all_to_all.34 = f32[2,1,1536]{2,1,0:T(1,128)S(1)} all-to-all(f32[2,1,1536]{2,1,0:T(1,128)S(1)} %reshape.53), channel_id=1, replica_groups=mesh['cosmo'=2,'shell'=4,'band_0'=16,'band_1'=2] {'band_1'}, dimensions={0} | all-to-all | bytes 24576 | tf_op jit(solution)/shard_map/all_to_all | solution.py:31
  111.3 0.5 broadcast.55
  111.8 0.7 reduce.1
  112.6 0.4 copy.40
  113.1 0.5 reshape.55
  113.6 14.0 %all_to_all.35 = f32[16,1,192]{2,1,0:T(1,128)S(1)} all-to-all(f32[16,1,192]{2,1,0:T(1,128)S(1)} %reshape.55), channel_id=1, replica_groups=mesh['cosmo'=2,'shell'=4,'band_0'=16,'band_1'=2] {'band_0'}, dimensions={0} | all-to-all | bytes 24576 | tf_op jit(solution)/shard_map/all_to_all | solution.py:31
  127.7 0.7 reduce.2
  128.3 0.6 reshape.56
  128.9 1.5 %copy.41 = f32[16,2,1,3,4,2,4]{6,1,0,5,4,3,2:T(2,128)S(1)} copy(f32[16,2,1,3,4,2,4]{4,1,6,5,3,2,0:T(2,128)S(1)} %bitcast.68) | data formatting | bytes 24576 | tf_op jit(solution)/shard_map/all_to_all | solution.py:31
  130.5 0.9 reshape.48
  (26 shorter events, 0.5 us)
Async XLA Ops:
  2.2 58.8 %all-to-all-start = ((f32[128,4,2,128]{0,2,1,3:T(2,128)}), f32[128,4,2,128]{0,2,1,3:T(2,128)S(1)}, u32[]{:S(2)}, u32[]{:S(2)}) async-start(f32[128,4,2,128]{0,2,1,3:T(2,128)} %copy.32), calls=%async_computation | async-start | bytes 1048576 | tf_op jit(solution)/shard_map/all_to_all | solution.py:48
  61.4 16.3 %copy-start = (f32[128,4096]{1,0:T(8,128)S(1)}, f32[128,4096]{1,0:T(8,128)}, u32[]{:S(2)}) copy-start(f32[128,4096]{1,0:T(8,128)} %param.13) | copy-start | bytes 6291460
  61.4 16.2 %copy-start.3 = (s32[4]{0:T(128)S(1)}, s32[4]{0:T(128)}, u32[]{:S(2)}) copy-start(s32[4]{0:T(128)} %param.15) | copy-start | bytes 52
  61.5 16.2 %copy-start.4 = (f32[128]{0:T(128)S(1)}, f32[128]{0:T(128)}, u32[]{:S(2)}) copy-start(f32[128]{0:T(128)} %param.14) | copy-start | bytes 1540
  61.5 24.8 %slice-start = ((s8[8388608]{0:T(1024)(128)(4,1)}), s8[4194304]{0:T(1024)(128)(4,1)S(1)}, s32[]{:S(2)}) async-start(s8[8388608]{0:T(1024)(128)(4,1)} %bitcast.64), calls=%async_computation.4 | async-start | bytes 8388608
  77.7 8.5 %slice-start.1 = ((s8[8388608]{0:T(1024)(128)(4,1)}), s8[4194304]{0:T(1024)(128)(4,1)S(1)}, s32[]{:S(2)}) async-start(s8[8388608]{0:T(1024)(128)(4,1)} %bitcast.64), calls=%async_computation.5 | async-start | bytes 8388608
  86.3 7.6 %copy-start.2 = (bf16[4,128,4096]{2,1,0:T(8,128)(2,1)S(1)}, bf16[4,128,4096]{2,1,0:T(8,128)(2,1)}, u32[]{:S(2)}) copy-start(bf16[4,128,4096]{2,1,0:T(8,128)(2,1)} %param.12) | copy-start | bytes 12582916
  86.3 8.9 %copy-start.1 = (bf16[4,128,4096]{2,1,0:T(8,128)(2,1)S(1)}, bf16[4,128,4096]{2,1,0:T(8,128)(2,1)}, u32[]{:S(2)}) copy-start(bf16[4,128,4096]{2,1,0:T(8,128)(2,1)} %param.11) | copy-start | bytes 12582916
where the time goes:
time: 132 us; the launch traced here: 131 us
  matrix products  34.9 us (26%)
  waiting for transfers between devices  32.6 us (25%)
  blocking collectives  27.8 us (21%)
  starting transfers between devices  25.5 us (19%)
  local copies, waits for them, and re-layouts  6.99 us (5%)
  other arithmetic  3.32 us (3%)
    all_to_all x1, waiting for transfers between devices, on_device(): lax.all_to_all(weighted, BAND, split_axis=3, concat_axis=1, tiled=True)  32.6 us
    all_to_all x1, starting transfers between devices, on_device(): lax.all_to_all(weighted, BAND, split_axis=3, concat_axis=1, tiled=True)  25.5 us
    all_to_all x2, blocking collectives, exchange_in_order(): lax.all_to_all(tiles, axes[k], split_axis=k, concat_axis=k, tiled=True)  19.3 us
    dot_general x1, matrix products, on_device(): jnp.einsum('nrcm,mrl->nmcl', lax.all_to_all(weighted, BAND, split_axis=3,...  16.2 us
    dot_general x1, matrix products, on_device(): jnp.einsum('bs,smcl->bmcl', efficiency, harmonic * window[:, None, None,...  8.51 us
    all_to_all x1, blocking collectives, sent_and_summed(): tiles = lax.all_to_all(cut_along(shard, dim, size), axis, 0, 0, tiled=True)  8.49 us
    dot_general x1, matrix products, on_device(): jnp.einsum('bmcl,mrl->brcm', binned, legendre, precision=highest, preferr...  7.56 us
  transfers between devices with their start and end apart: 1, of which 1 were waited for; matrix products, arithmetic and copies ran while one was open for 1% of the time, Pallas kernels for 0%

commit v1 on v0

v1 whole, which is shorter than its diff:
```python
import functools

import jax
import jax.numpy as jnp
from jax import lax
from jax.experimental import pallas as pl
from jax.experimental.pallas import tpu as pltpu
from jax.sharding import PartitionSpec as P

MESH = pl.DeviceIdType.MESH
LANES = 128
TILE = 256


def roll(x, shift, axis):
    return pltpu.roll(x, shift, axis)


def kernel(
    n_band,
    n_shell,
    modes,
    weight,
    legendre,
    plus,
    minus,
    window,
    lensing,
    source,
    out,
    modes_v,
    send_v,
    recv_v,
    leg_v,
    tab_v,
    win_v,
    eff_v,
    fac_v,
    a_v,
    x_v,
    h0_v,
    h1_v,
    w_v,
    p1s_v,
    p1r_v,
    p2t_v,
    p2s_v,
    p2r_v,
    in_sem,
    leg_sem,
    plus_sem,
    minus_sem,
    send_sem,
    recv_sem,
    p1s_sem,
    p1r_sem,
    p2s_sem,
    p2r_sem,
):
    f32, bf16 = jnp.float32, jnp.bfloat16
    band, shell = lax.axis_index("band"), lax.axis_index("shell")
    chips = n_band // 2
    chip, core = band // 2, band % 2
    own = legendre.shape[0]
    cycles = legendre.shape[1]
    degrees = legendre.shape[2]
    shells = window.shape[0]
    bins = n_shell
    rows = 2 * (cycles // n_band)

    def peer(j):
        k = j // 2
        step = ((k + 1) // 2) * (2 * (k % 2) - 1)
        return 2 * ((chip + step + chips) % chips) + (core + j) % 2

    get_modes = pltpu.make_async_copy(modes, modes_v, in_sem.at[0])
    get_window = pltpu.make_async_copy(window, win_v, in_sem.at[1])
    get_modes.start()

    barrier = pltpu.get_barrier_semaphore()

    @pl.loop(1, n_band)
    def _(j):
        pl.semaphore_signal(barrier, inc=1, device_id={"band": peer(j)}, device_id_type=MESH)

    for dx in range(1, n_shell):
        pl.semaphore_signal(
            barrier, inc=1, device_id={"shell": (shell + dx) % n_shell}, device_id_type=MESH
        )

    def get_legendre(i):
        return pltpu.make_async_copy(legendre.at[i], leg_v.at[i], leg_sem.at[i])

    def get_plus(i):
        at = pl.ds(2 * cycles, cycles)
        return pltpu.make_async_copy(plus.at[i], tab_v.at[i, at], plus_sem.at[i])

    def get_minus(i):
        at = pl.ds(3 * cycles, cycles)
        return pltpu.make_async_copy(minus.at[i], tab_v.at[i, at], minus_sem.at[i])

    for i in range(own):
        get_legendre(i).start()
    get_window.start()
    for i in range(own):
        get_plus(i).start()
        get_minus(i).start()

    get_modes.wait()
    for k in range(rows):
        block = modes_v[pl.ds(k, shells, stride=rows), :] * weight[k // 2]
        send_v[pl.ds(k, LANES, stride=rows), :] = block.T

    pl.semaphore_wait(barrier, n_band - 1 + n_shell - 1)

    def order_copy(i, d):
        return pltpu.make_async_remote_copy(
            src_ref=send_v.at[pl.ds(pl.multiple_of((own * d + i) * rows, rows), rows)],
            dst_ref=recv_v.at[pl.ds(pl.multiple_of((i * n_band + band) * rows, rows), rows)],
            send_sem=send_sem.at[i],
            recv_sem=recv_sem.at[i],
            device_id={"band": d},
            device_id_type=MESH,
        )

    @pl.loop(0, own)
    def _(i):
        @pl.loop(1, n_band)
        def _(j):
            order_copy(i, peer(j)).start()

        recv_v[pl.ds(pl.multiple_of((i * n_band + band) * rows, rows), rows), :] = send_v[
            pl.ds(pl.multiple_of((own * band + i) * rows, rows), rows), :
        ]

    def all_orders(i):
        n = (n_band - 1) * rows
        at = pl.ds(pl.multiple_of(i * n_band * rows, rows), n)
        return pltpu.make_async_remote_copy(
            src_ref=recv_v.at[at],
            dst_ref=recv_v.at[at],
            send_sem=send_sem.at[i],
            recv_sem=recv_sem.at[i],
            device_id={"band": peer(1)},
            device_id_type=MESH,
        )

    spread = jnp.broadcast_to(lensing[0:1, :], (LANES, LANES)).T
    shell_id = shell * shells + lax.broadcasted_iota(jnp.int32, (shells, LANES), 0)
    for b in range(bins):
        at = jnp.full((shells, LANES), source[b], jnp.int32)
        eff_v[b] = spread * jnp.maximum(at - shell_id, 0).astype(f32) / (at + 1).astype(f32)

    sub = lax.broadcasted_iota(jnp.int32, (8, LANES), 0)
    even = sub % 2 == 0

    @pl.loop(0, degrees // LANES)
    def _(k):
        at = pl.multiple_of(k * LANES, LANES)
        degree = (at + lax.broadcasted_iota(jnp.int32, (8, LANES), 1)).astype(f32)
        ratio = jnp.where(
            degree >= 2.0,
            jnp.sqrt((degree + 2.0) * (degree - 1.0) / jnp.maximum(degree * (degree + 1.0), 1.0)),
            0.0,
        )
        turned = jnp.where(even, ratio, -ratio)
        fac_v[:, pl.ds(at, LANES)] = jnp.where(
            sub < 2, 1.0, jnp.where(sub < 4, -ratio, turned)
        )

    @pl.loop(0, own)
    def _(i):
        get_legendre(i).wait()

        @pl.loop(0, cycles // 16)
        def _(k):
            at = pl.ds(pl.multiple_of(k * 16, 16), 16)
            value = leg_v[i, at, :]
            high = value.astype(bf16)
            tab_v[i, at, :] = high
            at = pl.ds(pl.multiple_of(cycles + k * 16, 16), 16)
            tab_v[i, at, :] = (value - high.astype(f32)).astype(bf16)

    get_window.wait()

    def transform(i, t, h_v):
        table = tab_v[i, 0 : 2 * cycles, pl.ds(pl.multiple_of(t * TILE, TILE), TILE)]
        h_v[...] = jnp.dot(a_v[...], table, preferred_element_type=f32) + jnp.dot(
            x_v[...], table[:cycles], preferred_element_type=f32
        )

    def bin_sums(t, h_v):
        for k in range(TILE // LANES):
            lanes = pl.ds(pl.multiple_of(t * TILE + k * LANES, LANES), LANES)
            sums = [[None, None] for _ in range(bins)]
            for g in range(shells // 8):
                at = slice(8 * g, 8 * g + 8)
                w = win_v[at, lanes]
                for c in range(2):
                    h = h_v[c * shells + 8 * g : c * shells + 8 * g + 8, k * LANES : (k + 1) * LANES]
                    hw = h * w
                    for b in range(bins):
                        term = hw * eff_v[b, at, :]
                        sums[b][c] = term if g == 0 else sums[b][c] + term
            fac = fac_v[:, lanes]
            parts = []
            for b in range(bins):
                x, y = sums[b]
                z = jnp.where(even, x + roll(x, 1, 0), y + roll(y, 1, 0))
                z = z + roll(z, 2, 0)
                z = z + roll(z, 4, 0)
                turned = roll(z, 1, 0)
                v = jnp.where((sub == 4) | (sub == 5), turned, z) * fac
                low = z - z.astype(bf16).astype(f32)
                parts.append(jnp.where(sub >= 6, low, v))
            w_v[:, lanes] = jnp.concatenate(parts, axis=0).astype(bf16)

    tiles = degrees // TILE
    chunk = 1024

    @pl.loop(0, own)
    def _(i):
        all_orders(i).wait_recv()
        for c in range(2):
            x = recv_v[pl.ds(i * n_band * rows + c, cycles, stride=2), :].T
            high = x.astype(bf16)
            at = slice(c * shells, (c + 1) * shells)
            a_v[at, :cycles] = high
            a_v[at, cycles:] = high
            x_v[at, :] = (x - high.astype(f32)).astype(bf16)

        transform(i, 0, h0_v)

        @pl.loop(0, tiles // 2 - 1)
        def _(t):
            transform(i, 2 * t + 1, h1_v)
            bin_sums(2 * t, h0_v)
            transform(i, 2 * t + 2, h0_v)
            bin_sums(2 * t + 1, h1_v)

        transform(i, tiles - 1, h1_v)
        bin_sums(tiles - 2, h0_v)
        bin_sums(tiles - 1, h1_v)

        get_plus(i).wait()
        get_minus(i).wait()
        maps = None
        for k in range(degrees // chunk):
            at = slice(k * chunk, (k + 1) * chunk)
            term = lax.dot_general(
                tab_v[i, :, at],
                w_v[:, at],
                (((1,), (1,)), ((), ())),
                preferred_element_type=f32,
            )
            maps = term if maps is None else maps + term
        maps = maps.T
        for b in range(bins):
            kh, kl, p, m = (
                maps[8 * b : 8 * b + 8, q * cycles : (q + 1) * cycles] for q in range(4)
            )
            p1s_v[i, b] = jnp.where(
                sub < 2, kh + kl + roll(kh, 2, 0), jnp.where(sub < 4, p, m)
            )
        for dx in range(1, n_shell):
            d = (shell + dx) % n_shell
            pltpu.make_async_remote_copy(
                src_ref=p1s_v.at[i, d],
                dst_ref=p1r_v.at[i, shell],
                send_sem=p1s_sem.at[i],
                recv_sem=p1r_sem.at[i],
                device_id={"shell": d},
                device_id_type=MESH,
            ).start()
        p1r_v[i, shell] = p1s_v[i, shell]

    def all_bins(i):
        return pltpu.make_async_remote_copy(
            src_ref=p1r_v.at[i, pl.ds(0, n_shell - 1)],
            dst_ref=p1r_v.at[i, pl.ds(0, n_shell - 1)],
            send_sem=p1s_sem.at[i],
            recv_sem=p1r_sem.at[i],
            device_id={"shell": (shell + 1) % n_shell},
            device_id_type=MESH,
        )

    summed = []
    for i in range(own):
        all_bins(i).wait_recv()
        total = p1r_v[i, 0]
        for x in range(1, n_shell):
            total = total + p1r_v[i, x]
        summed.append(total)
    width = 8 * own
    summed.append(jnp.zeros((LANES - width, LANES), f32))
    p2t_v[...] = jnp.concatenate(summed, axis=0).T
    per = cycles // n_band
    packed = p2t_v[pl.ds(0, n_band, stride=per), :]
    for q in range(1, per):
        packed = packed + roll(p2t_v[pl.ds(q, n_band, stride=per), :], q * width, 1)
    for d in range(n_band):
        p2s_v[d] = packed[d : d + 1]

    @pl.loop(1, n_band)
    def _(j):
        d = peer(n_band - j)
        pltpu.make_async_remote_copy(
            src_ref=p2s_v.at[d],
            dst_ref=p2r_v.at[band],
            send_sem=p2s_sem,
            recv_sem=p2r_sem,
            device_id={"band": d},
            device_id_type=MESH,
        ).start()

    p2r_v[band] = p2s_v[band]
    last = pltpu.make_async_remote_copy(
        src_ref=p2r_v.at[pl.ds(0, n_band - 1)],
        dst_ref=p2r_v.at[pl.ds(0, n_band - 1)],
        send_sem=p2s_sem,
        recv_sem=p2r_sem,
        device_id={"band": peer(1)},
        device_id_type=MESH,
    )
    last.wait_recv()
    got = jnp.concatenate(
        [p2r_v[d] for d in range(n_band)] + [jnp.zeros((LANES - n_band, LANES), f32)], axis=0
    ).T
    lane = lax.broadcasted_iota(jnp.int32, (8, LANES), 1)
    for q in range(per):
        field = jnp.zeros((8, LANES), f32)
        for i in range(own):
            block = got[(q * own + i) * 8 : (q * own + i) * 8 + 8]
            block = jnp.take_along_axis(block, lane // own, axis=1)
            field = jnp.where(lane % own == i, block, field)
        for f in range(3):
            at = f * 2 * per + 2 * q
            out[at : at + 2, :] = field[2 * f : 2 * f + 2]
    for i in range(own):
        all_orders(i).wait_send()
        all_bins(i).wait_send()
    last.wait_send()


def on_device(n_band, n_shell, modes, weight, legendre, plus, minus, window, lensing, source):
    f32, bf16 = jnp.float32, jnp.bfloat16
    own, cycles, degrees = legendre.shape
    shells, per, parts, orders = modes.shape
    rows = per * parts
    bins = n_shell
    vmem, smem, hbm = pltpu.VMEM, pltpu.SMEM, pl.ANY
    dma = pltpu.SemaphoreType.DMA
    maps = pl.pallas_call(
        functools.partial(kernel, n_band, n_shell),
        out_shape=jax.ShapeDtypeStruct((3 * rows, orders), f32),
        in_specs=[
            pl.BlockSpec(memory_space=hbm),
            pl.BlockSpec(memory_space=smem),
            pl.BlockSpec(memory_space=hbm),
            pl.BlockSpec(memory_space=hbm),
            pl.BlockSpec(memory_space=hbm),
            pl.BlockSpec(memory_space=hbm),
            pl.BlockSpec(memory_space=vmem),
            pl.BlockSpec(memory_space=smem),
        ],
        out_specs=pl.BlockSpec(memory_space=vmem),
        scratch_shapes=[
            vmem((shells * rows, orders), f32),
            vmem((orders * rows, shells), f32),
            vmem((orders * rows, shells), f32),
            vmem((own, cycles, degrees), f32),
            vmem((own, 4 * cycles, degrees), bf16),
            vmem((shells, degrees), f32),
            vmem((bins, shells, LANES), f32),
            vmem((8, degrees), f32),
            vmem((2 * shells, 2 * cycles), bf16),
            vmem((2 * shells, cycles), bf16),
            vmem((2 * shells, TILE), f32),
            vmem((2 * shells, TILE), f32),
            vmem((8 * bins, degrees), bf16),
            vmem((own, n_shell, 8, LANES), f32),
            vmem((own, n_shell, 8, LANES), f32),
            vmem((cycles, LANES), f32),
            vmem((n_band, 1, LANES), f32),
            vmem((n_band, 1, LANES), f32),
            dma((2,)),
            dma((own,)),
            dma((own,)),
            dma((own,)),
            dma((own,)),
            dma((own,)),
            dma((own,)),
            dma((own,)),
            dma,
            dma,
        ],
        compiler_params=pltpu.CompilerParams(
            collective_id=0, has_side_effects=True, vmem_limit_bytes=60 * 2**20
        ),
    )(
        modes.reshape(shells * rows, orders),
        weight,
        legendre,
        plus,
        minus,
        window,
        lensing.reshape(1, shells),
        source,
    )
    return maps.reshape(1, 3, per, parts, orders)


def solution(mesh):
    in_specs = (
        P(("cosmo", "shell"), "band", None, None),
        P("band"),
        P("band", None, None),
        P("band", None, None),
        P("band", None, None),
        P("shell", None),
        P(("cosmo", "shell")),
        P("cosmo"),
    )
    out_specs = P(("cosmo", "shell"), None, "band", None, None)
    return jax.shard_map(
        functools.partial(on_device, mesh.shape["band"], mesh.shape["shell"]),
        mesh=mesh,
        in_specs=in_specs,
        out_specs=out_specs,
        check_vma=False,
    )
```

time: 132 us -> 74.8 us (0.57)
  Pallas kernels: 0 us -> 73.3 us
  matrix products: 34.9 us -> 0 us
  waiting for transfers between devices: 32.6 us -> 0 us
  blocking collectives: 27.8 us -> 0 us
  starting transfers between devices: 25.5 us -> 0 us
  local copies, waits for them, and re-layouts: 6.99 us -> 1.31 us
  other arithmetic: 3.32 us -> 0 us
    pallas_call x0 -> x1, Pallas kernels: none -> 73.3 us  [on_device(): pl.pallas_call(functools.partial(kernel, n_band, n_shell), out_shape=jax....]
    dot_general x5 -> x0, matrix products: 34.9 us -> none  [the longest x1 16.2 us: on_device(): jnp.einsum('nrcm,mrl->nmcl', lax.all_to_all(weighted, BAND, split_axis=3,...]
    all_to_all x1 -> x0, waiting for transfers between devices: 32.6 us -> none  [on_device(): lax.all_to_all(weighted, BAND, split_axis=3, concat_axis=1, tiled=True)]
    all_to_all x3 -> x0, blocking collectives: 27.8 us -> none  [the longest x2 19.3 us: exchange_in_order(): lax.all_to_all(tiles, axes[k], split_axis=k, concat_axis=k, tiled=True)]
    all_to_all x1 -> x0, starting transfers between devices: 25.5 us -> none  [on_device(): lax.all_to_all(weighted, BAND, split_axis=3, concat_axis=1, tiled=True)]
    all_to_all x5 -> x0, local copies, waits for them, and re-layouts: 2.89 us -> none  [the longest x3 2.45 us: exchange_in_order(): lax.all_to_all(tiles, axes[k], split_axis=k, concat_axis=k, tiled=True)]
    reshape x4 -> x0, local copies, waits for them, and re-layouts: 1.65 us -> none  [the longest x1 0.86 us: laid_out(): return jnp.moveaxis(tiles, 0, dim).reshape(dims)]
    all_to_all x2 -> x0, other arithmetic: 1.37 us -> none  [exchange_in_order(): lax.all_to_all(tiles, axes[k], split_axis=k, concat_axis=k, tiled=True)]
  transfers between devices with their start and end apart: 1 -> 0, of which waited for: 1 -> 0; matrix products, arithmetic and copies ran while one was open for 1% -> 0% of each run, Pallas kernels for 0% -> 0%
where the time goes in v1:
time: 74.8 us; the launch traced here: 74.6 us
  Pallas kernels  73.3 us (98%)
  local copies, waits for them, and re-layouts  1.31 us (2%)
    pallas_call x1, Pallas kernels, on_device(): pl.pallas_call(functools.partial(kernel, n_band, n_shell), out_shape=jax....  73.3 us

profile of v1, /device:TPU:33, one launch (start us, length us, event | category | flops | bytes accessed | tf_op | source)
XLA Modules:
  0.0 74.6 jit_solution(1882521897157665115)
XLA Ops:
  0.0 73.3 %shard_map.82 = f32[24,128]{1,0:T(8,128)} custom-call(f32[1024,128]{1,0:T(8,128)} %bitcast.3, f32[4]{0:T(128)} %weight.1, f32[4,128,4096]{2,1,0:T(8,128)} %legendre.1, bf16[4,128,4096]{2,1,0:T(8,128)(2,1)} %plus.1, bf16[4,128,4096]{2,1,0:T(8,128)(2,1)} %minus.1, f32[128,4096]{1,0:T(8,128)} %window.1, f32[1,128]{1,0:T(1,128)} %bitcast.5, s32[4]{0:T(128)} %source.1), custom_call_target="tpu_custom_call" | custom-call | tf_op jit(solution)/shard_map/pallas_call | solution.py:353
  73.3 1.3 %copy.10 = f32[1,3,4,2,128]{4,3,2,1,0:T(2,128)} copy(f32[1,3,4,2,128]{4,3,2,1,0:T(2,128)} %bitcast.4) | data formatting | bytes 24576

commit v2 on v1

--- a/solution.py
+++ b/solution.py
@@ -9,7 +9,7 @@
 
 MESH = pl.DeviceIdType.MESH
 LANES = 128
-TILE = 256
+TILE = 512
 
 
 def roll(x, shift, axis):
@@ -41,11 +41,13 @@
     h0_v,
     h1_v,
     w_v,
+    m_v,
     p1s_v,
     p1r_v,
     p2t_v,
     p2s_v,
     p2r_v,
+    near_sem,
     in_sem,
     leg_sem,
     plus_sem,
@@ -77,16 +79,26 @@
     get_window = pltpu.make_async_copy(window, win_v, in_sem.at[1])
     get_modes.start()
 
+    def along(step, to):
+        return {"band": 2 * ((chip + step + chips) % chips) + to}
+
     barrier = pltpu.get_barrier_semaphore()
-
-    @pl.loop(1, n_band)
-    def _(j):
-        pl.semaphore_signal(barrier, inc=1, device_id={"band": peer(j)}, device_id_type=MESH)
-
-    for dx in range(1, n_shell):
-        pl.semaphore_signal(
-            barrier, inc=1, device_id={"shell": (shell + dx) % n_shell}, device_id_type=MESH
-        )
+    others = [{"shell": (shell + dx) % n_shell} for dx in range(1, n_shell)]
+    first = [along(1, core), along(-1, core), along(0, 1 - core)]
+    for d in first + others:
+        pl.semaphore_signal(barrier, inc=1, device_id=d, device_id_type=MESH)
+    pl.semaphore_wait(barrier, len(first + others))
+
+    def tell(level):
+        for sign in (1, -1):
+            pl.semaphore_signal(
+                near_sem.at[level],
+                inc=1,
+                device_id=along(sign * 2**level, core),
+                device_id_type=MESH,
+            )
+
+    tell(0)
 
     def get_legendre(i):
         return pltpu.make_async_copy(legendre.at[i], leg_v.at[i], leg_sem.at[i])
@@ -110,8 +122,6 @@
     for k in range(rows):
         block = modes_v[pl.ds(k, shells, stride=rows), :] * weight[k // 2]
         send_v[pl.ds(k, LANES, stride=rows), :] = block.T
-
-    pl.semaphore_wait(barrier, n_band - 1 + n_shell - 1)
 
     def order_copy(i, d):
         return pltpu.make_async_remote_copy(
@@ -123,12 +133,30 @@
             device_id_type=MESH,
         )
 
-    @pl.loop(0, own)
-    def _(i):
-        @pl.loop(1, n_band)
+    def send(begin, end, orders):
+        @pl.loop(begin, end)
         def _(j):
-            order_copy(i, peer(j)).start()
-
+            d = peer(j)
+            for i in orders:
+                order_copy(i, d).start()
+
+    levels = chips.bit_length() - 2
+    every = range(own)
+    reach = 2
+    for level in range(levels):
+        pl.semaphore_wait(near_sem.at[level], 2)
+        if level + 1 < levels:
+            tell(level + 1)
+        else:
+            pl.semaphore_signal(
+                near_sem.at[levels], inc=1, device_id=along(0, 1 - core), device_id_type=MESH
+            )
+            break
+        begin, reach = reach, 2 ** (level + 2) * 2 - 2
+        send(1 if level == 0 else begin, reach, every)
+    pl.semaphore_wait(near_sem.at[levels], 1)
+    for i in every:
+        send(reach, n_band, [i])
         recv_v[pl.ds(pl.multiple_of((i * n_band + band) * rows, rows), rows), :] = send_v[
             pl.ds(pl.multiple_of((own * band + i) * rows, rows), rows), :
         ]
@@ -163,10 +191,8 @@
             jnp.sqrt((degree + 2.0) * (degree - 1.0) / jnp.maximum(degree * (degree + 1.0), 1.0)),
             0.0,
         )
-        turned = jnp.where(even, ratio, -ratio)
-        fac_v[:, pl.ds(at, LANES)] = jnp.where(
-            sub < 2, 1.0, jnp.where(sub < 4, -ratio, turned)
-        )
+        fac_v[0:8, pl.ds(at, LANES)] = -ratio
+        fac_v[8:16, pl.ds(at, LANES)] = jnp.where(even, ratio, -ratio)
 
     @pl.loop(0, own)
     def _(i):
@@ -188,6 +214,12 @@
         h_v[...] = jnp.dot(a_v[...], table, preferred_element_type=f32) + jnp.dot(
             x_v[...], table[:cycles], preferred_element_type=f32
         )
+
+    def merge(x, y, s):
+        clear = (sub & s) == 0
+        if s == 4:
+            return jnp.where(clear, x, y) + roll(jnp.where(clear, y, x), 4, 0)
+        return jnp.where(clear, x, y) + jnp.where(clear, roll(x, 8 - s, 0), roll(y, s, 0))
 
     def bin_sums(t, h_v):
         for k in range(TILE // LANES):
@@ -202,21 +234,29 @@
                     for b in range(bins):
                         term = hw * eff_v[b, at, :]
                         sums[b][c] = term if g == 0 else sums[b][c] + term
-            fac = fac_v[:, lanes]
-            parts = []
-            for b in range(bins):
-                x, y = sums[b]
-                z = jnp.where(even, x + roll(x, 1, 0), y + roll(y, 1, 0))
-                z = z + roll(z, 2, 0)
-                z = z + roll(z, 4, 0)
-                turned = roll(z, 1, 0)
-                v = jnp.where((sub == 4) | (sub == 5), turned, z) * fac
-                low = z - z.astype(bf16).astype(f32)
-                parts.append(jnp.where(sub >= 6, low, v))
-            w_v[:, lanes] = jnp.concatenate(parts, axis=0).astype(bf16)
-
-    tiles = degrees // TILE
-    chunk = 1024
+            z = [[merge(sums[b][c], sums[b + 2][c], 4) for c in range(2)] for b in range(2)]
+            z = [merge(z[0][c], z[1][c], 2) for c in range(2)]
+            z = merge(z[0], z[1], 1)
+            low = z - z.astype(bf16).astype(f32)
+            turned = jnp.where(even, roll(z, 7, 0), roll(z, 1, 0))
+            w_v[:, lanes] = jnp.concatenate(
+                [z, low, z * fac_v[0:8, lanes], turned * fac_v[8:16, lanes]], axis=0
+            ).astype(bf16)
+
+    def products(i, t):
+        at = pl.ds(pl.multiple_of(t * 2 * TILE, 2 * TILE), 2 * TILE)
+        return lax.dot_general(
+            tab_v[i, :, at], w_v[:, at], (((1,), (1,)), ((), ())), preferred_element_type=f32
+        )
+
+    pairs = degrees // (2 * TILE)
+
+    def pair(i, t):
+        transform(i, 2 * t + 1, h1_v)
+        bin_sums(2 * t, h0_v)
+        if not isinstance(t, int) or t < pairs - 1:
+            transform(i, 2 * t + 2, h0_v)
+        bin_sums(2 * t + 1, h1_v)
 
     @pl.loop(0, own)
     def _(i):
@@ -229,39 +269,29 @@
             a_v[at, cycles:] = high
             x_v[at, :] = (x - high.astype(f32)).astype(bf16)
 
-        transform(i, 0, h0_v)
-
-        @pl.loop(0, tiles // 2 - 1)
-        def _(t):
-            transform(i, 2 * t + 1, h1_v)
-            bin_sums(2 * t, h0_v)
-            transform(i, 2 * t + 2, h0_v)
-            bin_sums(2 * t + 1, h1_v)
-
-        transform(i, tiles - 1, h1_v)
-        bin_sums(tiles - 2, h0_v)
-        bin_sums(tiles - 1, h1_v)
-
         get_plus(i).wait()
         get_minus(i).wait()
-        maps = None
-        for k in range(degrees // chunk):
-            at = slice(k * chunk, (k + 1) * chunk)
-            term = lax.dot_general(
-                tab_v[i, :, at],
-                w_v[:, at],
-                (((1,), (1,)), ((), ())),
-                preferred_element_type=f32,
+        transform(i, 0, h0_v)
+        pair(i, 0)
+        m_v[...] = jnp.zeros_like(m_v)
+
+        @pl.loop(1, pairs - 1)
+        def _(t):
+            m_v[...] += products(i, t - 1)
+            pair(i, t)
+
+        m_v[...] += products(i, pairs - 2)
+        pair(i, pairs - 1)
+        maps = (m_v[...] + products(i, pairs - 1)).T
+        field = [maps[:, q * cycles : (q + 1) * cycles] for q in range(4)]
+        kappa = field[0][0:8] + field[0][8:16] + field[1][0:8]
+        p, m = field[2][16:24], field[3][24:32]
+        for b in range(bins):
+            k0, p0, m0 = (
+                x if n % 8 == 0 else roll(x, n % 8, 0)
+                for x, n in ((kappa, 8 - 2 * b), (p, 10 - 2 * b), (m, 12 - 2 * b))
             )
-            maps = term if maps is None else maps + term
-        maps = maps.T
-        for b in range(bins):
-            kh, kl, p, m = (
-                maps[8 * b : 8 * b + 8, q * cycles : (q + 1) * cycles] for q in range(4)
-            )
-            p1s_v[i, b] = jnp.where(
-                sub < 2, kh + kl + roll(kh, 2, 0), jnp.where(sub < 4, p, m)
-            )
+            p1s_v[i, b] = jnp.where(sub < 2, k0, jnp.where(sub < 4, p0, m0))
         for dx in range(1, n_shell):
             d = (shell + dx) % n_shell
             pltpu.make_async_remote_copy(
@@ -372,17 +402,19 @@
             vmem((own, 4 * cycles, degrees), bf16),
             vmem((shells, degrees), f32),
             vmem((bins, shells, LANES), f32),
-            vmem((8, degrees), f32),
+            vmem((16, degrees), f32),
             vmem((2 * shells, 2 * cycles), bf16),
             vmem((2 * shells, cycles), bf16),
             vmem((2 * shells, TILE), f32),
             vmem((2 * shells, TILE), f32),
             vmem((8 * bins, degrees), bf16),
+            vmem((4 * cycles, 8 * bins), f32),
             vmem((own, n_shell, 8, LANES), f32),
             vmem((own, n_shell, 8, LANES), f32),
             vmem((cycles, LANES), f32),
             vmem((n_band, 1, LANES), f32),
             vmem((n_band, 1, LANES), f32),
+            pltpu.SemaphoreType.REGULAR((n_band.bit_length() - 2,)),
             dma((2,)),
             dma((own,)),
             dma((own,)),

time: 74.8 us -> 73.1 us (0.977)
  Pallas kernels: 73.3 us -> 71.1 us
    pallas_call x1, Pallas kernels: 73.3 us -> 71.1 us  [on_device(): pl.pallas_call(functools.partial(kernel, n_band, n_shell), out_shape=jax....]
where the time goes in v2:
time: 73.1 us; the launch traced here: 72.5 us
  Pallas kernels  71.1 us (97%)
  local copies, waits for them, and re-layouts  1.31 us (2%)
    pallas_call x1, Pallas kernels, on_device(): pl.pallas_call(functools.partial(kernel, n_band, n_shell), out_shape=jax....  71.1 us

profile of v2, /device:TPU:33, one launch (start us, length us, event | category | flops | bytes accessed | tf_op | source)
XLA Modules:
  0.0 72.5 jit_solution(17517762273554928360)
XLA Ops:
  0.0 71.1 %shard_map.82 = f32[24,128]{1,0:T(8,128)} custom-call(f32[1024,128]{1,0:T(8,128)} %bitcast.3, f32[4]{0:T(128)} %weight.1, f32[4,128,4096]{2,1,0:T(8,128)} %legendre.1, bf16[4,128,4096]{2,1,0:T(8,128)(2,1)} %plus.1, bf16[4,128,4096]{2,1,0:T(8,128)(2,1)} %minus.1, f32[128,4096]{1,0:T(8,128)} %window.1, f32[1,128]{1,0:T(1,128)} %bitcast.5, s32[4]{0:T(128)} %source.1), custom_call_target="tpu_custom_call" | custom-call | tf_op jit(solution)/shard_map/pallas_call | solution.py:383
  71.2 1.3 %copy.10 = f32[1,3,4,2,128]{4,3,2,1,0:T(2,128)} copy(f32[1,3,4,2,128]{4,3,2,1,0:T(2,128)} %bitcast.4) | data formatting | bytes 24576

commit v3 on v2

--- a/solution.py
+++ b/solution.py
@@ -28,6 +28,9 @@
     lensing,
     source,
     out,
+    weight_v,
+    lensing_v,
+    source_v,
     modes_v,
     send_v,
     recv_v,
@@ -78,27 +81,37 @@
     get_modes = pltpu.make_async_copy(modes, modes_v, in_sem.at[0])
     get_window = pltpu.make_async_copy(window, win_v, in_sem.at[1])
     get_modes.start()
-
-    def along(step, to):
-        return {"band": 2 * ((chip + step + chips) % chips) + to}
+    get_small = [
+        pltpu.make_async_copy(x, y, in_sem.at[2 + k])
+        for k, (x, y) in enumerate(((weight, weight_v), (lensing, lensing_v), (source, source_v)))
+    ]
+    for copy in get_small:
+        copy.start()
+
+    near = chips // 4
+    reach = 4 * near + 2
 
     barrier = pltpu.get_barrier_semaphore()
-    others = [{"shell": (shell + dx) % n_shell} for dx in range(1, n_shell)]
-    first = [along(1, core), along(-1, core), along(0, 1 - core)]
-    for d in first + others:
-        pl.semaphore_signal(barrier, inc=1, device_id=d, device_id_type=MESH)
-    pl.semaphore_wait(barrier, len(first + others))
-
-    def tell(level):
-        for sign in (1, -1):
-            pl.semaphore_signal(
-                near_sem.at[level],
-                inc=1,
-                device_id=along(sign * 2**level, core),
-                device_id_type=MESH,
-            )
-
-    tell(0)
+
+    @pl.loop(0, reach - 1)
+    def _(j):
+        pl.semaphore_signal(
+            barrier, inc=1, device_id={"band": peer(reach - 1 - j)}, device_id_type=MESH
+        )
+
+    for dx in range(1, n_shell):
+        pl.semaphore_signal(
+            barrier, inc=1, device_id={"shell": (shell + dx) % n_shell}, device_id_type=MESH
+        )
+    pl.semaphore_wait(barrier, reach - 1 + n_shell - 1)
+
+    for step in (near, -near):
+        pl.semaphore_signal(
+            near_sem,
+            inc=1,
+            device_id={"band": 2 * ((chip + step + chips) % chips) + core},
+            device_id_type=MESH,
+        )
 
     def get_legendre(i):
         return pltpu.make_async_copy(legendre.at[i], leg_v.at[i], leg_sem.at[i])
@@ -119,8 +132,11 @@
         get_minus(i).start()
 
     get_modes.wait()
+    for copy in get_small:
+        copy.wait()
     for k in range(rows):
-        block = modes_v[pl.ds(k, shells, stride=rows), :] * weight[k // 2]
+        scale = jnp.broadcast_to(weight_v[0:1, k // 2 : k // 2 + 1], (shells, LANES))
+        block = modes_v[pl.ds(k, shells, stride=rows), :] * scale
         send_v[pl.ds(k, LANES, stride=rows), :] = block.T
 
     def order_copy(i, d):
@@ -134,29 +150,19 @@
         )
 
     def send(begin, end, orders):
-        @pl.loop(begin, end)
-        def _(j):
-            d = peer(j)
+        @pl.loop(0, end - begin)
+        def _(k):
+            d = peer(end - 1 - k)
             for i in orders:
                 order_copy(i, d).start()
 
-    levels = chips.bit_length() - 2
     every = range(own)
-    reach = 2
-    for level in range(levels):
-        pl.semaphore_wait(near_sem.at[level], 2)
-        if level + 1 < levels:
-            tell(level + 1)
-        else:
-            pl.semaphore_signal(
-                near_sem.at[levels], inc=1, device_id=along(0, 1 - core), device_id_type=MESH
-            )
-            break
-        begin, reach = reach, 2 ** (level + 2) * 2 - 2
-        send(1 if level == 0 else begin, reach, every)
-    pl.semaphore_wait(near_sem.at[levels], 1)
+    early = own // 2
+    send(1, reach, range(early))
+    pl.semaphore_wait(near_sem, 2)
     for i in every:
-        send(reach, n_band, [i])
+        send(reach if i < early else 1, n_band, [i])
+    for i in every:
         recv_v[pl.ds(pl.multiple_of((i * n_band + band) * rows, rows), rows), :] = send_v[
             pl.ds(pl.multiple_of((own * band + i) * rows, rows), rows), :
         ]
@@ -173,10 +179,10 @@
             device_id_type=MESH,
         )
 
-    spread = jnp.broadcast_to(lensing[0:1, :], (LANES, LANES)).T
+    spread = jnp.broadcast_to(lensing_v[0:1, :], (LANES, LANES)).T
     shell_id = shell * shells + lax.broadcasted_iota(jnp.int32, (shells, LANES), 0)
     for b in range(bins):
-        at = jnp.full((shells, LANES), source[b], jnp.int32)
+        at = jnp.broadcast_to(source_v[0:1, b : b + 1], (shells, LANES))
         eff_v[b] = spread * jnp.maximum(at - shell_id, 0).astype(f32) / (at + 1).astype(f32)
 
     sub = lax.broadcasted_iota(jnp.int32, (8, LANES), 0)
@@ -378,23 +384,17 @@
     shells, per, parts, orders = modes.shape
     rows = per * parts
     bins = n_shell
-    vmem, smem, hbm = pltpu.VMEM, pltpu.SMEM, pl.ANY
+    vmem, hbm = pltpu.VMEM, pl.ANY
     dma = pltpu.SemaphoreType.DMA
     maps = pl.pallas_call(
         functools.partial(kernel, n_band, n_shell),
-        out_shape=jax.ShapeDtypeStruct((3 * rows, orders), f32),
-        in_specs=[
-            pl.BlockSpec(memory_space=hbm),
-            pl.BlockSpec(memory_space=smem),
-            pl.BlockSpec(memory_space=hbm),
-            pl.BlockSpec(memory_space=hbm),
-            pl.BlockSpec(memory_space=hbm),
-            pl.BlockSpec(memory_space=hbm),
-            pl.BlockSpec(memory_space=vmem),
-            pl.BlockSpec(memory_space=smem),
-        ],
+        out_shape=vmem((3 * rows, orders), f32),
+        in_specs=[pl.BlockSpec(memory_space=hbm)] * 8,
         out_specs=pl.BlockSpec(memory_space=vmem),
         scratch_shapes=[
+            vmem((1, per), f32),
+            vmem((1, shells), f32),
+            vmem((1, bins), jnp.int32),
             vmem((shells * rows, orders), f32),
             vmem((orders * rows, shells), f32),
             vmem((orders * rows, shells), f32),
@@ -414,8 +414,8 @@
             vmem((cycles, LANES), f32),
             vmem((n_band, 1, LANES), f32),
             vmem((n_band, 1, LANES), f32),
-            pltpu.SemaphoreType.REGULAR((n_band.bit_length() - 2,)),
-            dma((2,)),
+            pltpu.SemaphoreType.REGULAR,
+            dma((5,)),
             dma((own,)),
             dma((own,)),
             dma((own,)),
@@ -431,13 +431,13 @@
         ),
     )(
         modes.reshape(shells * rows, orders),
-        weight,
+        weight.reshape(1, per),
         legendre,
         plus,
         minus,
         window,
         lensing.reshape(1, shells),
-        source,
+        source.reshape(1, bins),
     )
     return maps.reshape(1, 3, per, parts, orders)
 

time: 73.1 us -> 67.6 us (0.925)
  Pallas kernels: 71.1 us -> 66.9 us
    pallas_call x1, Pallas kernels: 71.1 us -> 66.9 us  [on_device(): pl.pallas_call(functools.partial(kernel, n_band, n_shell), out_shape=vmem...]
where the time goes in v3:
time: 67.6 us; the launch traced here: 67.5 us
  Pallas kernels  66.9 us (99%)
    pallas_call x1, Pallas kernels, on_device(): pl.pallas_call(functools.partial(kernel, n_band, n_shell), out_shape=vmem...  66.9 us

profile of v3, /device:TPU:33, one launch (start us, length us, event | category | flops | bytes accessed | tf_op | source)
XLA Modules:
  0.0 67.5 jit_solution(9684477995699693802)
XLA Ops:
  0.0 66.9 %shard_map.82 = f32[24,128]{1,0:T(8,128)S(1)} custom-call(f32[1024,128]{1,0:T(8,128)} %bitcast.6, f32[1,4]{1,0:T(1,128)} %bitcast.7, f32[4,128,4096]{2,1,0:T(8,128)} %legendre.1, bf16[4,128,4096]{2,1,0:T(8,128)(2,1)} %plus.1, bf16[4,128,4096]{2,1,0:T(8,128)(2,1)} %minus.1, f32[128,4096]{1,0:T(8,128)} %window.1, f32[1,128]{1,0:T(1,128)} %bitcast.8, ...), custom_call_target="tpu_custom_call" | custom-call | tf_op jit(solution)/shard_map/pallas_call | solution.py:389
  66.9 0.6 copy.10

commit v4 on v3

--- a/solution.py
+++ b/solution.py
@@ -74,9 +74,9 @@
     rows = 2 * (cycles // n_band)
 
     def peer(j):
-        k = j // 2
-        step = ((k + 1) // 2) * (2 * (k % 2) - 1)
-        return 2 * ((chip + step + chips) % chips) + (core + j) % 2
+        k = lax.div(j, 2)
+        step = lax.div(k + 1, 2) * (2 * lax.rem(k, 2) - 1)
+        return 2 * lax.rem(chip + step + chips, chips) + lax.rem(core + j, 2)
 
     get_modes = pltpu.make_async_copy(modes, modes_v, in_sem.at[0])
     get_window = pltpu.make_async_copy(window, win_v, in_sem.at[1])
@@ -134,48 +134,53 @@
     get_modes.wait()
     for copy in get_small:
         copy.wait()
-    for k in range(rows):
-        scale = jnp.broadcast_to(weight_v[0:1, k // 2 : k // 2 + 1], (shells, LANES))
-        block = modes_v[pl.ds(k, shells, stride=rows), :] * scale
-        send_v[pl.ds(k, LANES, stride=rows), :] = block.T
-
-    def order_copy(i, d):
+    per = rows // 2
+    for r in range(per):
+        scale = jnp.broadcast_to(weight_v[0:1, r : r + 1], (shells, LANES))
+        for c in range(2):
+            block = modes_v[pl.ds(2 * r + c, shells, stride=rows), :] * scale
+            send_v[pl.ds(c * per + r, LANES, stride=rows), :] = block.T
+
+    def order_copy(i, d, c=None):
+        n, skip = (rows, 0) if c is None else (per, c * per)
         return pltpu.make_async_remote_copy(
-            src_ref=send_v.at[pl.ds(pl.multiple_of((own * d + i) * rows, rows), rows)],
-            dst_ref=recv_v.at[pl.ds(pl.multiple_of((i * n_band + band) * rows, rows), rows)],
+            src_ref=send_v.at[pl.ds(pl.multiple_of((own * d + i) * rows + skip, n), n)],
+            dst_ref=recv_v.at[pl.ds(pl.multiple_of((i * n_band + band) * rows + skip, n), n)],
             send_sem=send_sem.at[i],
-            recv_sem=recv_sem.at[i],
+            recv_sem=recv_sem.at[i if c is None else i + c],
             device_id={"band": d},
             device_id_type=MESH,
         )
 
-    def send(begin, end, orders):
+    def send(begin, end, orders, c=None):
         @pl.loop(0, end - begin)
         def _(k):
             d = peer(end - 1 - k)
             for i in orders:
-                order_copy(i, d).start()
-
-    every = range(own)
+                order_copy(i, d, c).start()
+
+    final = own - 1
     early = own // 2
     send(1, reach, range(early))
     pl.semaphore_wait(near_sem, 2)
-    for i in every:
+    for i in range(final):
         send(reach if i < early else 1, n_band, [i])
-    for i in every:
+    for c in range(2):
+        send(1, n_band, [final], c)
+    for i in range(own):
         recv_v[pl.ds(pl.multiple_of((i * n_band + band) * rows, rows), rows), :] = send_v[
             pl.ds(pl.multiple_of((own * band + i) * rows, rows), rows), :
         ]
 
-    def all_orders(i):
-        n = (n_band - 1) * rows
+    def all_orders(i, c=None):
+        n = (n_band - 1) * (rows if c is None else per)
         at = pl.ds(pl.multiple_of(i * n_band * rows, rows), n)
         return pltpu.make_async_remote_copy(
             src_ref=recv_v.at[at],
             dst_ref=recv_v.at[at],
             send_sem=send_sem.at[i],
-            recv_sem=recv_sem.at[i],
-            device_id={"band": peer(1)},
+            recv_sem=recv_sem.at[i if c is None else i + c],
+            device_id={"band": 2 * chip + 1 - core},
             device_id_type=MESH,
         )
 
@@ -215,11 +220,12 @@
 
     get_window.wait()
 
-    def transform(i, t, h_v):
+    def transform(i, t, h_v, cs):
         table = tab_v[i, 0 : 2 * cycles, pl.ds(pl.multiple_of(t * TILE, TILE), TILE)]
-        h_v[...] = jnp.dot(a_v[...], table, preferred_element_type=f32) + jnp.dot(
-            x_v[...], table[:cycles], preferred_element_type=f32
-        )
+        h = jnp.dot(a_v[...], table, preferred_element_type=f32)
+        if len(cs) == 2:
+            h = h + jnp.dot(x_v[...], table[:cycles], preferred_element_type=f32)
+        h_v[...] = h
 
     def merge(x, y, s):
         clear = (sub & s) == 0
@@ -227,22 +233,26 @@
             return jnp.where(clear, x, y) + roll(jnp.where(clear, y, x), 4, 0)
         return jnp.where(clear, x, y) + jnp.where(clear, roll(x, 8 - s, 0), roll(y, s, 0))
 
-    def bin_sums(t, h_v):
+    def bin_sums(t, h_v, cs):
         for k in range(TILE // LANES):
             lanes = pl.ds(pl.multiple_of(t * TILE + k * LANES, LANES), LANES)
-            sums = [[None, None] for _ in range(bins)]
+            here = slice(k * LANES, (k + 1) * LANES)
+            sums = [[None] * len(cs) for _ in range(bins)]
             for g in range(shells // 8):
                 at = slice(8 * g, 8 * g + 8)
+                after = slice(shells + 8 * g, shells + 8 * g + 8)
                 w = win_v[at, lanes]
-                for c in range(2):
-                    h = h_v[c * shells + 8 * g : c * shells + 8 * g + 8, k * LANES : (k + 1) * LANES]
+                hs = [h_v[at, here], h_v[after, here]]
+                if len(cs) == 1:
+                    hs = [hs[0] + hs[1]]
+                for c, h in enumerate(hs):
                     hw = h * w
                     for b in range(bins):
                         term = hw * eff_v[b, at, :]
                         sums[b][c] = term if g == 0 else sums[b][c] + term
-            z = [[merge(sums[b][c], sums[b + 2][c], 4) for c in range(2)] for b in range(2)]
-            z = [merge(z[0][c], z[1][c], 2) for c in range(2)]
-            z = merge(z[0], z[1], 1)
+            z = [[merge(x, y, 4) for x, y in zip(sums[b], sums[b + 2])] for b in range(2)]
+            z = [merge(x, y, 2) for x, y in zip(*z)]
+            z = merge(z[0], z[-1], 1)
             low = z - z.astype(bf16).astype(f32)
             turned = jnp.where(even, roll(z, 7, 0), roll(z, 1, 0))
             w_v[:, lanes] = jnp.concatenate(
@@ -257,41 +267,59 @@
 
     pairs = degrees // (2 * TILE)
 
-    def pair(i, t):
-        transform(i, 2 * t + 1, h1_v)
-        bin_sums(2 * t, h0_v)
+    def pair(i, t, cs):
+        transform(i, 2 * t + 1, h1_v, cs)
+        bin_sums(2 * t, h0_v, cs)
         if not isinstance(t, int) or t < pairs - 1:
-            transform(i, 2 * t + 2, h0_v)
-        bin_sums(2 * t + 1, h1_v)
-
-    @pl.loop(0, own)
-    def _(i):
-        all_orders(i).wait_recv()
-        for c in range(2):
-            x = recv_v[pl.ds(i * n_band * rows + c, cycles, stride=2), :].T
+            transform(i, 2 * t + 2, h0_v, cs)
+        bin_sums(2 * t + 1, h1_v, cs)
+
+    def part_of(i, c, cs):
+        tiles = []
+        for q in range(n_band // 2):
+            at = i * n_band * rows + 2 * rows * q
+            if len(cs) == 1:
+                at = at + c * per
+                tiles.append(recv_v[pl.ds(at, per), :])
+                tiles.append(recv_v[pl.ds(at + rows, per), :])
+                continue
+            at = pl.multiple_of(at, 2 * rows)
+            x, y = recv_v[pl.ds(at, rows), :], recv_v[pl.ds(at + rows, rows), :]
+            if c == 0:
+                tiles.append(jnp.where(sub < per, x, roll(y, per, 0)))
+            else:
+                tiles.append(jnp.where(sub < per, roll(x, per, 0), y))
+        return jnp.concatenate(tiles, axis=0).T
+
+    def work(i, cs):
+        for k, c in enumerate(cs):
+            x = part_of(i, c, cs)
             high = x.astype(bf16)
-            at = slice(c * shells, (c + 1) * shells)
+            low = (x - high.astype(f32)).astype(bf16)
+            at = slice(k * shells, (k + 1) * shells)
             a_v[at, :cycles] = high
             a_v[at, cycles:] = high
-            x_v[at, :] = (x - high.astype(f32)).astype(bf16)
-
-        get_plus(i).wait()
-        get_minus(i).wait()
-        transform(i, 0, h0_v)
-        pair(i, 0)
+            if len(cs) == 2:
+                x_v[at, :] = low
+            else:
+                a_v[shells:, :cycles] = low
+                a_v[shells:, cycles:] = low
+        transform(i, 0, h0_v, cs)
+        pair(i, 0, cs)
         m_v[...] = jnp.zeros_like(m_v)
 
         @pl.loop(1, pairs - 1)
         def _(t):
             m_v[...] += products(i, t - 1)
-            pair(i, t)
+            pair(i, t, cs)
 
         m_v[...] += products(i, pairs - 2)
-        pair(i, pairs - 1)
+        pair(i, pairs - 1, cs)
         maps = (m_v[...] + products(i, pairs - 1)).T
         field = [maps[:, q * cycles : (q + 1) * cycles] for q in range(4)]
-        kappa = field[0][0:8] + field[0][8:16] + field[1][0:8]
-        p, m = field[2][16:24], field[3][24:32]
+        return field[0][0:8] + field[0][8:16] + field[1][0:8], field[2][16:24], field[3][24:32]
+
+    def give(i, kappa, p, m):
         for b in range(bins):
             k0, p0, m0 = (
                 x if n % 8 == 0 else roll(x, n % 8, 0)
@@ -310,6 +338,26 @@
             ).start()
         p1r_v[i, shell] = p1s_v[i, shell]
 
+    @pl.loop(0, final)
+    def _(i):
+        all_orders(i).wait_recv()
+        get_plus(i).wait()
+        get_minus(i).wait()
+        give(i, *work(i, (0, 1)))
+
+    get_plus(final).wait()
+    get_minus(final).wait()
+    all_orders(final, 0).wait_recv()
+    real = work(final, (0,))
+    all_orders(final, 1).wait_recv()
+    imag = work(final, (1,))
+    give(
+        final,
+        jnp.where(even, real[0], imag[0]),
+        jnp.where(even, real[1], imag[1]),
+        jnp.where(even, imag[2], real[2]),
+    )
+
     def all_bins(i):
         return pltpu.make_async_remote_copy(
             src_ref=p1r_v.at[i, pl.ds(0, n_shell - 1)],
@@ -330,7 +378,6 @@
     width = 8 * own
     summed.append(jnp.zeros((LANES - width, LANES), f32))
     p2t_v[...] = jnp.concatenate(summed, axis=0).T
-    per = cycles // n_band
     packed = p2t_v[pl.ds(0, n_band, stride=per), :]
     for q in range(1, per):
         packed = packed + roll(p2t_v[pl.ds(q, n_band, stride=per), :], q * width, 1)
@@ -355,7 +402,7 @@
         dst_ref=p2r_v.at[pl.ds(0, n_band - 1)],
         send_sem=p2s_sem,
         recv_sem=p2r_sem,
-        device_id={"band": peer(1)},
+        device_id={"band": 2 * chip + 1 - core},
         device_id_type=MESH,
     )
     last.wait_recv()
@@ -420,7 +467,7 @@
             dma((own,)),
             dma((own,)),
             dma((own,)),
-            dma((own,)),
+            dma((own + 1,)),
             dma((own,)),
             dma((own,)),
             dma,

time: 67.6 us -> 69.2 us (1.024)
  Pallas kernels: 66.9 us -> 68.5 us
    pallas_call x1, Pallas kernels: 66.9 us -> 68.5 us  [on_device(): pl.pallas_call(functools.partial(kernel, n_band, n_shell), out_shape=vmem...]
where the time goes in v4:
time: 69.2 us; the launch traced here: 69.1 us
  Pallas kernels  68.5 us (99%)
    pallas_call x1, Pallas kernels, on_device(): pl.pallas_call(functools.partial(kernel, n_band, n_shell), out_shape=vmem...  68.5 us

profile of v4, /device:TPU:33, one launch (start us, length us, event | category | flops | bytes accessed | tf_op | source)
XLA Modules:
  0.0 69.1 jit_solution(11643255073528027039)
XLA Ops:
  0.0 68.5 %shard_map.82 = f32[24,128]{1,0:T(8,128)S(1)} custom-call(f32[1024,128]{1,0:T(8,128)} %bitcast.6, f32[1,4]{1,0:T(1,128)} %bitcast.7, f32[4,128,4096]{2,1,0:T(8,128)} %legendre.1, bf16[4,128,4096]{2,1,0:T(8,128)(2,1)} %plus.1, bf16[4,128,4096]{2,1,0:T(8,128)(2,1)} %minus.1, f32[128,4096]{1,0:T(8,128)} %window.1, f32[1,128]{1,0:T(1,128)} %bitcast.8, ...), custom_call_target="tpu_custom_call" | custom-call | tf_op jit(solution)/shard_map/pallas_call | solution.py:436
  68.5 0.6 copy.10

commit v5 on v3

--- a/solution.py
+++ b/solution.py
@@ -74,9 +74,9 @@
     rows = 2 * (cycles // n_band)
 
     def peer(j):
-        k = j // 2
-        step = ((k + 1) // 2) * (2 * (k % 2) - 1)
-        return 2 * ((chip + step + chips) % chips) + (core + j) % 2
+        k = lax.div(j, 2)
+        step = lax.div(k + 1, 2) * (2 * lax.rem(k, 2) - 1)
+        return 2 * lax.rem(chip + step + chips, chips) + lax.rem(core + j, 2)
 
     get_modes = pltpu.make_async_copy(modes, modes_v, in_sem.at[0])
     get_window = pltpu.make_async_copy(window, win_v, in_sem.at[1])
@@ -103,15 +103,6 @@
         pl.semaphore_signal(
             barrier, inc=1, device_id={"shell": (shell + dx) % n_shell}, device_id_type=MESH
         )
-    pl.semaphore_wait(barrier, reach - 1 + n_shell - 1)
-
-    for step in (near, -near):
-        pl.semaphore_signal(
-            near_sem,
-            inc=1,
-            device_id={"band": 2 * ((chip + step + chips) % chips) + core},
-            device_id_type=MESH,
-        )
 
     def get_legendre(i):
         return pltpu.make_async_copy(legendre.at[i], leg_v.at[i], leg_sem.at[i])
@@ -138,6 +129,16 @@
         scale = jnp.broadcast_to(weight_v[0:1, k // 2 : k // 2 + 1], (shells, LANES))
         block = modes_v[pl.ds(k, shells, stride=rows), :] * scale
         send_v[pl.ds(k, LANES, stride=rows), :] = block.T
+
+    pl.semaphore_wait(barrier, reach - 1 + n_shell - 1)
+
+    for step in (near, -near):
+        pl.semaphore_signal(
+            near_sem,
+            inc=1,
+            device_id={"band": 2 * ((chip + step + chips) % chips) + core},
+            device_id_type=MESH,
+        )
 
     def order_copy(i, d):
         return pltpu.make_async_remote_copy(
@@ -175,7 +176,7 @@
             dst_ref=recv_v.at[at],
             send_sem=send_sem.at[i],
             recv_sem=recv_sem.at[i],
-            device_id={"band": peer(1)},
+            device_id={"band": 2 * chip + 1 - core},
             device_id_type=MESH,
         )
 
@@ -298,8 +299,8 @@
                 for x, n in ((kappa, 8 - 2 * b), (p, 10 - 2 * b), (m, 12 - 2 * b))
             )
             p1s_v[i, b] = jnp.where(sub < 2, k0, jnp.where(sub < 4, p0, m0))
-        for dx in range(1, n_shell):
-            d = (shell + dx) % n_shell
+        for dx in sorted(range(1, n_shell), key=lambda x: abs(2 * x - n_shell)):
+            d = lax.rem(shell + dx, n_shell)
             pltpu.make_async_remote_copy(
                 src_ref=p1s_v.at[i, d],
                 dst_ref=p1r_v.at[i, shell],
@@ -355,7 +356,7 @@
         dst_ref=p2r_v.at[pl.ds(0, n_band - 1)],
         send_sem=p2s_sem,
         recv_sem=p2r_sem,
-        device_id={"band": peer(1)},
+        device_id={"band": 2 * chip + 1 - core},
         device_id_type=MESH,
     )
     last.wait_recv()

time: 67.6 us -> 67.6 us (level)
  no operation moved by 1% of the time
where the time goes in v5:
time: 67.6 us; the launch traced here: 67.5 us
  Pallas kernels  66.9 us (99%)
    pallas_call x1, Pallas kernels, on_device(): pl.pallas_call(functools.partial(kernel, n_band, n_shell), out_shape=vmem...  66.9 us

profile of v5, /device:TPU:33, one launch (start us, length us, event | category | flops | bytes accessed | tf_op | source)
XLA Modules:
  0.0 67.5 jit_solution(8884864800698350647)
XLA Ops:
  0.0 66.9 %shard_map.82 = f32[24,128]{1,0:T(8,128)S(1)} custom-call(f32[1024,128]{1,0:T(8,128)} %bitcast.6, f32[1,4]{1,0:T(1,128)} %bitcast.7, f32[4,128,4096]{2,1,0:T(8,128)} %legendre.1, bf16[4,128,4096]{2,1,0:T(8,128)(2,1)} %plus.1, bf16[4,128,4096]{2,1,0:T(8,128)(2,1)} %minus.1, f32[128,4096]{1,0:T(8,128)} %window.1, f32[1,128]{1,0:T(1,128)} %bitcast.8, ...), custom_call_target="tpu_custom_call" | custom-call | tf_op jit(solution)/shard_map/pallas_call | solution.py:390
  66.9 0.6 copy.10
